TPU v7x, 32 devices: a whole 2x2x4 slice. The times are simulated.
32 devices in a mesh: dp: 4 (over z), seq: 4 (over x, core), tensor: 2 (over y).
Axes of the slice: x: 2, y: 2, z: 4, core: 2. Of those that a mesh axis runs over, the one named last changes fastest.
Arguments:
- latent_embed: bfloat16 [20480, 2, 1024], P(('dp', 'seq'), None, 'tensor'), may hold values from -6 to 6
- adapter: bfloat16 [2, 1024, 1024], P(None, 'tensor'), may hold values from -0.125 to 0.125
- first_gain: float32 [1024], replicated, may hold values from 0.5 to 1.5
- query_weight: bfloat16 [1024, 1024], P(None, 'tensor'), may hold values from -0.1875 to 0.1875
- key_weight: bfloat16 [1024, 1024], P(None, 'tensor'), may hold values from -0.1875 to 0.1875
- value_weight: bfloat16 [1024, 1024], P(None, 'tensor'), may hold values from -0.1875 to 0.1875
- output_weight: bfloat16 [1024, 1024], P('tensor'), may hold values from -0.1875 to 0.1875
- second_gain: float32 [1024], replicated, may hold values from 0.5 to 1.5
- third_gain: float32 [1024], replicated, may hold values from 0.5 to 1.5
- gate_weight: bfloat16 [1024, 2816], P(None, 'tensor'), may hold values from -0.1875 to 0.1875
- up_weight: bfloat16 [1024, 2816], P(None, 'tensor'), may hold values from -0.1875 to 0.1875
- down_weight: bfloat16 [2816, 1024], P('tensor'), may hold values from -0.109375 to 0.109375
- fourth_gain: float32 [1024], replicated, may hold values from 0.5 to 1.5
- parents: int32 [4, 20], P('dp'), may hold values from -1 to 19, as said below
- positions: int32 [20480], P(('dp', 'seq')), may hold values from 0 to 2559, as said below
- cotangent: bfloat16 [20480, 1024], P(('dp', 'seq')), may hold values from -6 to 6
Outputs:
- layer_out: float32 [20480, 1024], P(('dp', 'seq'))
- latent_gradient: float32 [20480, 2, 1024], P(('dp', 'seq'), None, 'tensor')
- adapter_gradient: float32 [2, 1024, 1024], P(None, 'tensor')
- first_gain_gradient: float32 [1024], replicated
- query_gradient: float32 [1024, 1024], P(None, 'tensor')
- key_gradient: float32 [1024, 1024], P(None, 'tensor')
- value_gradient: float32 [1024, 1024], P(None, 'tensor')
- output_gradient: float32 [1024, 1024], P('tensor')
- second_gain_gradient: float32 [1024], replicated
- third_gain_gradient: float32 [1024], replicated
- gate_gradient: float32 [1024, 2816], P(None, 'tensor')
- up_gradient: float32 [1024, 2816], P(None, 'tensor')
- down_gradient: float32 [2816, 1024], P('tensor')
- fourth_gain_gradient: float32 [1024], replicated
Inputs may be any that keep to these rules, and one draw needn't show every extreme that they name: `parents`: each tree's segments form a trunk of 8 chained segments from the root, 4 branches whose parent is the trunk's last segment and 2 leaves under each branch; which segment number plays which role is drawn. `positions`: a token's position is 256 times the number of its segment's ancestors plus its place inside its segment.
All inputs are finite; a program needn't handle non-finite values.
Results may differ from a plain program's by a relative error of at most 0.025.
Values may be sent and summed in bfloat16 or wider, within the bound.
A program may use at most 896 MiB of HBM per device.

v0:
```python
import jax
import jax.numpy as jnp
from jax import lax
from jax.sharding import PartitionSpec as P

DH = 64
SEG = 256
EPSILON = 1e-06
THETA = 50000.0


def normalize(values, gain):
    scale = lax.rsqrt(jnp.mean(values * values, axis=-1, keepdims=True) + EPSILON)
    normed = values * scale
    return (normed * gain, normed, scale)


def normalize_back(upstream, gain, normed, scale):
    scaled = upstream * gain
    inward = scale * (scaled - normed * jnp.mean(scaled * normed, axis=-1, keepdims=True))
    return (inward, jnp.sum(upstream * normed, axis=0))


def angles(positions, width):
    half = width // 2
    freq = THETA ** (-jnp.arange(half, dtype=jnp.float32) * 2.0 / width)
    angle = positions.astype(jnp.float32)[:, None] * freq[None, :]
    return (jnp.cos(angle)[:, None, :], jnp.sin(angle)[:, None, :])


def rotate(values, cosine, sine, sign):
    half = values.shape[-1] // 2
    first = values[..., :half]
    second = values[..., half:]
    return jnp.concatenate(
        [first * cosine - sign * second * sine, second * cosine + sign * first * sine], axis=-1
    )


def ancestry(parent_row):
    labels = jnp.arange(parent_row.shape[0], dtype=jnp.int32)

    def extend(index, state):
        current, total = state
        total = total | (current[:, None] == labels[None, :])
        current = jnp.where(current >= 0, jnp.take(parent_row, jnp.maximum(current, 0)), -1)
        return (current, total)

    start = (parent_row, jnp.zeros((parent_row.shape[0], parent_row.shape[0]), jnp.bool_))
    current, total = lax.fori_loop(0, parent_row.shape[0], extend, start)
    return total


def path_mask(parent_row, query_ids, key_ids):
    table = ancestry(parent_row)
    query_seg = query_ids // SEG
    key_seg = key_ids // SEG
    far = jnp.take(jnp.take(table, query_seg, axis=0), key_seg, axis=1)
    near = (query_seg[:, None] == key_seg[None, :]) & (key_ids[None, :] <= query_ids[:, None])
    return far | near


def on_device(
    latent_embed,
    adapter,
    first_gain,
    query_weight,
    key_weight,
    value_weight,
    output_weight,
    second_gain,
    third_gain,
    gate_weight,
    up_weight,
    down_weight,
    fourth_gain,
    parents,
    positions,
    cotangent,
):
    rows = latent_embed.shape[0]
    local_heads = query_weight.shape[1] // DH
    scale = DH ** (-0.5)
    adapted = lax.psum(
        jnp.einsum("rcd,cde->re", latent_embed, adapter, preferred_element_type=jnp.float32),
        "tensor",
    )
    first_out, first_normed, first_scale = normalize(adapted, first_gain)
    first_low = first_out.astype(jnp.bfloat16)
    cosine, sine = angles(positions, DH)
    query_raw = jnp.dot(first_low, query_weight, preferred_element_type=jnp.float32).reshape(
        rows, local_heads, DH
    )
    queries = rotate(query_raw, cosine, sine, 1.0).astype(jnp.bfloat16)
    key_raw = jnp.dot(first_low, key_weight, preferred_element_type=jnp.float32).reshape(
        rows, local_heads, DH
    )
    keys_local = rotate(key_raw, cosine, sine, 1.0).astype(jnp.bfloat16)
    values_local = (
        jnp.dot(first_low, value_weight, preferred_element_type=jnp.float32)
        .astype(jnp.bfloat16)
        .reshape(rows, local_heads, DH)
    )
    keys_all, values_all = (
        lax.all_gather(keys_local, "seq", axis=0, tiled=True),
        lax.all_gather(values_local, "seq", axis=0, tiled=True),
    )
    tree_rows = keys_all.shape[0]
    query_ids = lax.axis_index("seq") * rows + jnp.arange(rows, dtype=jnp.int32)
    key_ids = jnp.arange(tree_rows, dtype=jnp.int32)
    allowed = path_mask(parents[0], query_ids, key_ids)[None]

    def score_block(keys):
        raw = jnp.einsum("qhd,khd->hqk", queries, keys, preferred_element_type=jnp.float32) * scale
        return jnp.where(allowed, raw, -1e30)

    scores = score_block(keys_all)
    top = jnp.max(scores, axis=-1, keepdims=True)
    weights = jnp.exp(scores - top)
    total = jnp.sum(weights, axis=-1, keepdims=True)
    probs = weights / total
    logsum = top + jnp.log(total)
    attended = jnp.einsum(
        "hqk,khd->qhd", probs.astype(jnp.bfloat16), values_all, preferred_element_type=jnp.float32
    )
    attended = attended.reshape(rows, local_heads * DH).astype(jnp.bfloat16)
    attention = lax.psum(
        jnp.dot(attended, output_weight, preferred_element_type=jnp.float32).astype(jnp.bfloat16),
        "tensor",
    ).astype(jnp.float32)
    second_out, second_normed, second_scale = normalize(attention, second_gain)
    middle = adapted + second_out
    third_out, third_normed, third_scale = normalize(middle, third_gain)
    third_low = third_out.astype(jnp.bfloat16)
    gate = jnp.dot(third_low, gate_weight, preferred_element_type=jnp.float32)
    upward = jnp.dot(third_low, up_weight, preferred_element_type=jnp.float32)
    hidden = (jax.nn.silu(gate) * upward).astype(jnp.bfloat16)
    mixed = lax.psum(
        jnp.dot(hidden, down_weight, preferred_element_type=jnp.float32).astype(jnp.bfloat16),
        "tensor",
    ).astype(jnp.float32)
    fourth_out, fourth_normed, fourth_scale = normalize(mixed, fourth_gain)
    layer_out = middle + fourth_out
    upstream = cotangent.astype(jnp.float32)
    mixed_back, fourth_gain_part = normalize_back(
        upstream, fourth_gain, fourth_normed, fourth_scale
    )
    mixed_low = mixed_back.astype(jnp.bfloat16)
    down_part = jnp.einsum("rf,rd->fd", hidden, mixed_low, preferred_element_type=jnp.float32)
    hidden_back = (
        jnp.einsum("rd,fd->rf", mixed_low, down_weight, preferred_element_type=jnp.float32)
        .astype(jnp.bfloat16)
        .astype(jnp.float32)
    )
    swiglu_value, product_back = jax.vjp(
        lambda left, right: jax.nn.silu(left) * right, gate, upward
    )
    gate_back, up_back = product_back(hidden_back)
    gate_low = gate_back.astype(jnp.bfloat16)
    up_low = up_back.astype(jnp.bfloat16)
    gate_part = jnp.einsum("rd,rf->df", third_low, gate_low, preferred_element_type=jnp.float32)
    up_part = jnp.einsum("rd,rf->df", third_low, up_low, preferred_element_type=jnp.float32)
    third_term = jnp.einsum(
        "rf,df->rd", gate_low, gate_weight, preferred_element_type=jnp.float32
    ) + jnp.einsum("rf,df->rd", up_low, up_weight, preferred_element_type=jnp.float32)
    third_back = lax.psum(third_term.astype(jnp.bfloat16), "tensor").astype(jnp.float32)
    middle_part, third_gain_part = normalize_back(third_back, third_gain, third_normed, third_scale)
    middle_back = upstream + middle_part
    attention_back, second_gain_part = normalize_back(
        middle_back, second_gain, second_normed, second_scale
    )
    attention_low = attention_back.astype(jnp.bfloat16)
    output_part = jnp.einsum(
        "re,rd->ed", attended, attention_low, preferred_element_type=jnp.float32
    )
    attended_back = (
        jnp.einsum("rd,ed->re", attention_low, output_weight, preferred_element_type=jnp.float32)
        .astype(jnp.bfloat16)
        .reshape(rows, local_heads, DH)
    )
    keys_back, values_back = (
        lax.all_gather(keys_local, "seq", axis=0, tiled=True),
        lax.all_gather(values_local, "seq", axis=0, tiled=True),
    )
    probs_back = jnp.exp(score_block(keys_back) - logsum)
    prob_grad = jnp.einsum(
        "qhd,khd->hqk", attended_back, values_back, preferred_element_type=jnp.float32
    )
    score_grad = (
        probs_back * (prob_grad - jnp.sum(prob_grad * probs_back, axis=-1, keepdims=True))
    ).astype(jnp.bfloat16)
    query_rot = (
        jnp.einsum("hqk,khd->qhd", score_grad, keys_back, preferred_element_type=jnp.float32)
        * scale
    )
    key_rot_all = (
        jnp.einsum("hqk,qhd->khd", score_grad, queries, preferred_element_type=jnp.float32) * scale
    )
    value_back_all = jnp.einsum(
        "hqk,qhd->khd",
        probs_back.astype(jnp.bfloat16),
        attended_back,
        preferred_element_type=jnp.float32,
    )
    key_rot, value_back = (
        lax.psum_scatter(
            key_rot_all.astype(jnp.bfloat16), "seq", scatter_dimension=0, tiled=True
        ).astype(jnp.float32),
        lax.psum_scatter(
            value_back_all.astype(jnp.bfloat16), "seq", scatter_dimension=0, tiled=True
        ).astype(jnp.float32),
    )
    query_low = (
        rotate(query_rot, cosine, sine, -1.0).astype(jnp.bfloat16).reshape(rows, local_heads * DH)
    )
    key_low = (
        rotate(key_rot, cosine, sine, -1.0).astype(jnp.bfloat16).reshape(rows, local_heads * DH)
    )
    value_low = value_back.astype(jnp.bfloat16).reshape(rows, local_heads * DH)
    query_part = jnp.einsum("rd,re->de", first_low, query_low, preferred_element_type=jnp.float32)
    key_part = jnp.einsum("rd,re->de", first_low, key_low, preferred_element_type=jnp.float32)
    value_part = jnp.einsum("rd,re->de", first_low, value_low, preferred_element_type=jnp.float32)
    first_term = jnp.einsum(
        "re,de->rd", query_low, query_weight, preferred_element_type=jnp.float32
    )
    first_term = first_term + jnp.einsum(
        "re,de->rd", key_low, key_weight, preferred_element_type=jnp.float32
    )
    first_term = first_term + jnp.einsum(
        "re,de->rd", value_low, value_weight, preferred_element_type=jnp.float32
    )
    first_back = lax.psum(first_term.astype(jnp.bfloat16), "tensor").astype(jnp.float32)
    adapted_part, first_gain_part = normalize_back(
        first_back, first_gain, first_normed, first_scale
    )
    adapted_low = (middle_back + adapted_part).astype(jnp.bfloat16)
    latent_gradient = jnp.einsum(
        "re,cde->rcd", adapted_low, adapter, preferred_element_type=jnp.float32
    )
    adapter_part = jnp.einsum(
        "rcd,re->cde", latent_embed, adapted_low, preferred_element_type=jnp.float32
    )
    summed = (
        lax.psum(gate_part.astype(jnp.bfloat16), ("dp", "seq")).astype(jnp.float32),
        lax.psum(up_part.astype(jnp.bfloat16), ("dp", "seq")).astype(jnp.float32),
        lax.psum(down_part.astype(jnp.bfloat16), ("dp", "seq")).astype(jnp.float32),
        lax.psum(third_gain_part.astype(jnp.bfloat16), ("dp", "seq")).astype(jnp.float32),
        lax.psum(fourth_gain_part.astype(jnp.bfloat16), ("dp", "seq")).astype(jnp.float32),
        lax.psum(query_part.astype(jnp.bfloat16), ("dp", "seq")).astype(jnp.float32),
        lax.psum(key_part.astype(jnp.bfloat16), ("dp", "seq")).astype(jnp.float32),
        lax.psum(value_part.astype(jnp.bfloat16), ("dp", "seq")).astype(jnp.float32),
        lax.psum(output_part.astype(jnp.bfloat16), ("dp", "seq")).astype(jnp.float32),
        lax.psum(first_gain_part.astype(jnp.bfloat16), ("dp", "seq")).astype(jnp.float32),
        lax.psum(second_gain_part.astype(jnp.bfloat16), ("dp", "seq")).astype(jnp.float32),
        lax.psum(adapter_part.astype(jnp.bfloat16), ("dp", "seq")).astype(jnp.float32),
    )
    gate_total, up_total, down_total, third_total, fourth_total = (
        summed[0],
        summed[1],
        summed[2],
        summed[3],
        summed[4],
    )
    query_total, key_total, value_total, output_total, first_total, second_total = (
        summed[5],
        summed[6],
        summed[7],
        summed[8],
        summed[9],
        summed[10],
    )
    adapter_total = summed[11]
    return (
        layer_out,
        latent_gradient,
        adapter_total,
        first_total,
        query_total,
        key_total,
        value_total,
        output_total,
        second_total,
        third_total,
        gate_total,
        up_total,
        down_total,
        fourth_total,
    )


def solution(mesh):
    in_specs = (
        P(("dp", "seq"), None, "tensor"),
        P(None, "tensor", None),
        P(),
        P(None, "tensor"),
        P(None, "tensor"),
        P(None, "tensor"),
        P("tensor", None),
        P(),
        P(),
        P(None, "tensor"),
        P(None, "tensor"),
        P("tensor", None),
        P(),
        P("dp", None),
        P(("dp", "seq")),
        P(("dp", "seq"), None),
    )
    out_specs = (
        P(("dp", "seq"), None),
        P(("dp", "seq"), None, "tensor"),
        P(None, "tensor", None),
        P(),
        P(None, "tensor"),
        P(None, "tensor"),
        P(None, "tensor"),
        P("tensor", None),
        P(),
        P(),
        P(None, "tensor"),
        P(None, "tensor"),
        P("tensor", None),
        P(),
    )
    return jax.shard_map(
        on_device, mesh=mesh, in_specs=in_specs, out_specs=out_specs, check_vma=False
    )
```

profile of v0, /device:TPU:0, one launch (start us, length us, event | category | flops | bytes accessed | tf_op | source)
XLA Modules:
  0.0 1609.6 jit_solution(6540593411886035098)
XLA Ops:
  7.2 7.8 convolution_bitcast_fusion
  17.1 131.4 %all-reduce.9.cloned.1.call-done = f32[1280,1024]{1,0:T(8,128)} async-done(((f32[1280,1024]{1,0:T(8,128)}), f32[1280,1024]{1,0:T(8,128)}) %all-reduce.9.cloned.1.call-update) | async-done | bytes 5242896 | tf_op jit(solution)/shard_map/psum | solution.py:84
  160.6 16.5 %while.13 = (s32[]{:T(128)}, s32[20]{0:T(128)S(1)}, pred[20,20]{1,0:T(8,128)(4,1)S(1)}, s32[20]{0:T(128)S(1)}, s32[]{:T(128)}, /*index=5*/s32[]{:T(128)}) while((s32[]{:T(128)}, s32[20]{0:T(128)S(1)}, pred[20,20]{1,0:T(8,128)(4,1)S(1)}, s32[20]{0:T(128)S(1)}, s32[]{:T(128)}, /*index=5*/s32[]{:T(128)}) %tuple.77), condition=%wide.region_3.0_spmd.clone, body=%wide.region_2.3_spmd.clone.sunk | while | flops 2347 | bytes 5775 | solution.py:50
  180.3 22.2 %gather_fusion.2 = pred[5120,1280]{1,0:T(8,128)(4,1)} fusion(pred[1280,20]{0,1:T(8,128)(4,1)S(1)} %copy.38, s32[5120]{0:T(1024)S(1)} %broadcast_clamp_fusion), kind=kCustom, calls=%fused_computation.2 | custom fusion | bytes 13127680 | tf_op jit(solution)/shard_map/jit(_take)/gather | solution.py:58
  202.5 11.1 fusion.10
  213.6 16.6 %copy.39 = pred[1280,5120]{1,0:T(8,128)(4,1)} copy(pred[1280,5120]{0,1:T(8,128)(4,1)} %fusion.10) | data formatting | bytes 13107200 | tf_op jit(solution)/shard_map/or | solution.py:60
  235.0 74.7 %fusion.76 = (f32[8,1280]{1,0:T(8,128)}, f32[8,1280,5120]{2,1,0:T(8,128)}) fusion(bf16[5120,8,64]{0,2,1:T(8,128)(2,1)} %all-gather.5.cloned.1.call-done, bf16[1280,8,32]{0,2,1:T(8,128)(2,1)} %get-tuple-element.126, bf16[1280,8,32]{0,2,1:T(8,128)(2,1)S(1)} %copy-done.20, pred[1280,5120]{1,0:T(8,128)(4,1)} %copy.39), kind=kOutput, calls=%fused_computation.170 | convolution fusion | flops 6870784000 | bytes 222863360 | tf_op jit(solution)/shard_map/qhd,khd->hqk/dot_general | solution.py:114
  309.7 63.5 %fusion.3 = f32[8,1280]{1,0:T(8,128)S(1)} fusion(f32[8,1280,5120]{2,1,0:T(8,128)} %get-tuple-element.137, f32[8,1280]{1,0:T(8,128)} %get-tuple-element.136), kind=kLoop, calls=%fused_computation.16 | loop fusion | flops 104847360 | bytes 209797120 | tf_op jit(solution)/shard_map/reduce_sum | solution.py:120
  373.2 68.2 %fusion.56 = bf16[8,64,1280]{2,1,0:T(8,128)(2,1)} fusion(bf16[5120,8,64]{0,2,1:T(8,128)(2,1)} %all-gather.3.cloned.1.call-done, f32[8,1280,5120]{2,1,0:T(8,128)} %get-tuple-element.137, f32[8,1280]{1,0:T(8,128)S(1)} %fusion.3, f32[8,1280]{1,0:T(8,128)S(1)} %copy-done.43), kind=kOutput, calls=%fused_computation.97 | convolution fusion | flops 6868828160 | bytes 216350720 | tf_op jit(solution)/shard_map/hqk,khd->qhd/dot_general | solution.py:123
  446.4 74.6 %all-reduce.11.cloned.1.call-done = bf16[1280,1024]{1,0:T(8,128)(2,1)} async-done(((bf16[1280,1024]{1,0:T(8,128)(2,1)}), bf16[1280,1024]{1,0:T(8,128)(2,1)}) %all-reduce.11.cloned.1.call-update) | async-done | bytes 2621456 | tf_op jit(solution)/shard_map/psum | solution.py:127
  535.4 6.6 multiply_convert_fusion.2
  543.9 5.5 convolution_convert_fusion.5
  549.9 74.0 %all-reduce.13.cloned.1.call-done = bf16[1280,1024]{1,0:T(8,128)(2,1)} async-done(((bf16[1280,1024]{1,0:T(8,128)(2,1)}), bf16[1280,1024]{1,0:T(8,128)(2,1)}) %all-reduce.13.cloned.1.call-update) | async-done | bytes 2621456 | tf_op jit(solution)/shard_map/psum | solution.py:138
  630.7 11.4 fusion.14
  646.4 5.7 add_convert_fusion.1
  652.3 8.8 convolution_convert_fusion.3
  661.1 6.0 convolution_convert_fusion.2
  667.1 59.6 %all-reduce.15.cloned.1.call-done = bf16[1280,1024]{1,0:T(8,128)(2,1)} async-done(((bf16[1280,1024]{1,0:T(8,128)(2,1)}), bf16[1280,1024]{1,0:T(8,128)(2,1)}) %all-reduce.15.cloned.1.call-update) | async-done | bytes 2621456 | tf_op jit(solution)/shard_map/psum | solution.py:166
  726.7 5.6 fusion.52
  732.3 8.5 fusion.47
  744.7 138.2 %multiply_reduce_fusion = (f32[8,1280]{1,0:T(8,128)S(1)}, f32[8,1280,5120]{2,1,0:T(8,128)}) fusion(f32[8,1280,5120]{2,1,0:T(8,128)} %get-tuple-element.137, f32[8,1280]{1,0:T(8,128)S(1)} %log_add_fusion, bf16[1280,8,64]{0,2,1:T(8,128)(2,1)S(1)} %bitcast.82, bf16[5120,8,64]{0,2,1:T(8,128)(2,1)} %all-gather.3.cloned.1.call-done), kind=kOutput, calls=%fused_computation.11 | convolution fusion | flops 6868162560 | bytes 426065920 | tf_op jit(solution)/shard_map/qhd,khd->hqk/dot_general | solution.py:186
  882.9 160.8 %multiply_convert_fusion = bf16[8,1280,5120]{2,1,0:T(8,128)(2,1)} fusion(f32[8,1280,5120]{2,1,0:T(8,128)} %get-tuple-element.141, f32[8,1280,5120]{2,1,0:T(8,128)} %get-tuple-element.137, f32[8,1280]{1,0:T(8,128)S(1)} %get-tuple-element.140, f32[8,1280]{1,0:T(8,128)S(1)} %log_add_fusion), kind=kLoop, calls=%fused_computation.10 | loop fusion | flops 209715200 | bytes 524369920 | tf_op jit(solution)/shard_map/convert_element_type | solution.py:191
  1043.7 37.6 %fusion.55 = bf16[5120,8,64]{0,2,1:T(8,128)(2,1)} fusion(bf16[8,1280,5120]{2,1,0:T(8,128)(2,1)} %multiply_convert_fusion, bf16[1280,8,32]{0,2,1:T(8,128)(2,1)S(1)} %copy-done.22, bf16[1280,8,32]{0,2,1:T(8,128)(2,1)S(1)} %copy-done.21), kind=kOutput, calls=%fused_computation.82 | convolution fusion | flops 6718750720 | bytes 111411200 | tf_op jit(solution)/shard_map/hqk,qhd->khd/dot_general | solution.py:197
  1082.6 71.0 %fusion.19 = bf16[5120,8,64]{0,2,1:T(8,128)(2,1)} fusion(bf16[1280,8,64]{0,2,1:T(8,128)(2,1)S(1)} %bitcast.83, f32[8,1280,5120]{2,1,0:T(8,128)} %get-tuple-element.137, f32[8,1280]{1,0:T(8,128)S(1)} %log_add_fusion), kind=kOutput, calls=%fused_computation.40 | convolution fusion | flops 6818365440 | bytes 216309760 | tf_op jit(solution)/shard_map/hqk,qhd->khd/dot_general | solution.py:199
  1153.6 44.4 %multiply_bitcast_fusion = f32[1280,8,64]{0,2,1:T(8,128)S(1)} fusion(bf16[5120,8,64]{0,2,1:T(8,128)(2,1)} %all-gather.5.cloned.1.call-done, bf16[8,1280,5120]{2,1,0:T(8,128)(2,1)} %multiply_convert_fusion), kind=kOutput, calls=%fused_computation.99 | convolution fusion | flops 6711541760 | bytes 112721920 | tf_op jit(solution)/shard_map/hqk,khd->qhd/dot_general | solution.py:193
  1210.0 7.9 add_convert_fusion
  1218.0 8.0 convolution_convert_fusion.4
  1236.3 56.2 %all-reduce.17.cloned.1.call-done = bf16[1280,1024]{1,0:T(8,128)(2,1)} async-done(((bf16[1280,1024]{1,0:T(8,128)(2,1)}), bf16[1280,1024]{1,0:T(8,128)(2,1)}) %all-reduce.17.cloned.1.call-update) | async-done | bytes 2621456 | tf_op jit(solution)/shard_map/psum | solution.py:232
  1292.5 5.0 fusion.53
  1308.8 36.3 %all-reduce = (bf16[1024]{0:T(1024)(128)(2,1)S(1)}, bf16[1024]{0:T(1024)(128)(2,1)S(1)}, bf16[1024]{0:T(1024)(128)(2,1)S(1)}, bf16[1024]{0:T(1024)(128)(2,1)S(1)}) all-reduce(bf16[1024]{0:T(1024)(128)(2,1)S(1)} %get-tuple-element.91, bf16[1024]{0:T(1024)(128)(2,1)S(1)} %copy-done.52, ...), channel_id=1, replica_groups=mesh['dp'=4,'seq'=4,'tensor'=2] {'dp','seq'}, use_global_device_ids=true, to_apply=%region_22.23 | all-reduce | flops 4096 | bytes 16384 | tf_op jit(solution)/shard_map/psum | solution.py:253
  1352.1 10.7 copy.42
  1362.8 219.9 %all-reduce.19.cloned.1.call-done = (bf16[2,512,1024]{1,2,0:T(8,128)(2,1)}, bf16[1024,512]{1,0:T(8,128)(2,1)}, bf16[1024,512]{1,0:T(8,128)(2,1)}, bf16[1024,512]...) async-done(((bf16[2,512,1024]{1,2,0:T(8,128)(2,1)}, ...) | async-done | bytes 14942224 | tf_op jit(solution)/shard_map/psum | solution.py:255
  (333 shorter events, 136.4 us)
Async XLA Ops:
  7.2 536.7 %copy-start = (bf16[1408,1024]{1,0:T(8,128)(2,1)S(1)}, bf16[1408,1024]{1,0:T(8,128)(2,1)}, u32[]{:S(2)}) copy-start(bf16[1408,1024]{1,0:T(8,128)(2,1)} %param.29) | copy-start | bytes 8650756
  7.2 141.2 %all-reduce.9.cloned.1.call-start = ((), (), s32[]{:S(2)}) async-start(), calls=%async_computation.2 | async-start | bytes 10485760 | tf_op jit(solution)/shard_map/psum | solution.py:84
  15.0 136.5 %copy-start.48 = (f32[1024]{0:T(1024)S(1)}, f32[1024]{0:T(1024)}, u32[]{:S(2)}) copy-start(f32[1024]{0:T(1024)} %param.20) | copy-start | bytes 12292
  15.1 219.9 %all-gather.5.cloned.1.call-start = ((), (), s32[]{:S(2)}) async-start(), calls=%async_computation.4 | async-start | bytes 6553600 | tf_op jit(solution)/shard_map/all_gather | solution.py:105
  17.1 140.3 %copy-start.31 = (f32[1280,32]{0,1:T(8,128)}, f32[1280,32]{0,1:T(8,128)S(1)}, u32[]{:S(2)}) copy-start(f32[1280,32]{0,1:T(8,128)S(1)} %get-tuple-element.135) | copy-start | bytes 491524
  160.4 212.8 %all-gather.3.cloned.1.call-start = ((), (), s32[]{:S(2)}) async-start(), calls=%async_computation.3 | async-start | bytes 6553600 | tf_op jit(solution)/shard_map/all_gather | solution.py:106
  234.9 286.1 %all-reduce.11.cloned.1.call-start = ((), (), s32[]{:S(2)}) async-start(), calls=%async_computation.5 | async-start | bytes 5242880 | tf_op jit(solution)/shard_map/psum | solution.py:127
  309.7 63.5 %copy-start.43 = (f32[8,1280]{1,0:T(8,128)S(1)}, f32[8,1280]{1,0:T(8,128)}, u32[]{:S(2)}) copy-start(f32[8,1280]{1,0:T(8,128)} %get-tuple-element.136) | copy-start | bytes 122884
  446.1 77.4 %copy-start.47 = (f32[1024]{0:T(1024)S(1)}, f32[1024]{0:T(1024)}, u32[]{:S(2)}) copy-start(f32[1024]{0:T(1024)} %param.25) | copy-start | bytes 12292
  446.1 177.8 %all-reduce.13.cloned.1.call-start = ((), (), s32[]{:S(2)}) async-start(), calls=%async_computation.6 | async-start | bytes 5242880 | tf_op jit(solution)/shard_map/psum | solution.py:138
  535.4 6.6 copy-start.68
  549.4 77.0 %copy-start.50 = (f32[1024]{0:T(1024)S(1)}, f32[1024]{0:T(1024)}, u32[]{:S(2)}) copy-start(f32[1024]{0:T(1024)} %param.30) | copy-start | bytes 12292
  549.4 177.2 %all-reduce.15.cloned.1.call-start = ((), (), s32[]{:S(2)}) async-start(), calls=%async_computation.7 | async-start | bytes 5242880 | tf_op jit(solution)/shard_map/psum | solution.py:166
  623.9 6.8 copy-start.15
  630.7 11.4 copy-start.56
  652.2 545.9 %reduce-scatter.3.cloned.1.call-start = ((), (), s32[]{:S(2)}) async-start(), calls=%async_computation.8 | async-start | bytes 6553600 | tf_op jit(solution)/shard_map/reduce_scatter | solution.py:206
  652.2 8.9 copy-start.11
  652.2 8.9 copy-start.16
  652.3 8.9 copy-start.70
  667.1 65.2 %copy-start.9 = (bf16[1280,1024]{1,0:T(8,128)(2,1)S(1)}, bf16[1280,1024]{1,0:T(8,128)(2,1)}, u32[]{:S(2)}) copy-start(bf16[1280,1024]{1,0:T(8,128)(2,1)} %all-reduce.11.cloned.1.call-done) | copy-start | bytes 7864324
  744.7 138.2 %copy-start.3 = (bf16[1280,512]{0,1:T(8,128)(2,1)}, bf16[1280,512]{0,1:T(8,128)(2,1)S(1)}, u32[]{:S(2)}) copy-start(bf16[1280,512]{0,1:T(8,128)(2,1)S(1)} %convolution_convert_fusion.6) | copy-start | bytes 3932164
  882.9 160.8 %copy-start.21 = (bf16[1280,8,32]{0,2,1:T(8,128)(2,1)S(1)}, bf16[1280,8,32]{0,2,1:T(8,128)(2,1)}, u32[]{:S(2)}) copy-start(bf16[1280,8,32]{0,2,1:T(8,128)(2,1)} %get-tuple-element.125) | copy-start | bytes 1966084
  882.9 160.8 %copy-start.22 = (bf16[1280,8,32]{0,2,1:T(8,128)(2,1)S(1)}, bf16[1280,8,32]{0,2,1:T(8,128)(2,1)}, u32[]{:S(2)}) copy-start(bf16[1280,8,32]{0,2,1:T(8,128)(2,1)} %get-tuple-element.126) | copy-start | bytes 1966084
  1081.3 128.7 %reduce-scatter.5.cloned.1.call-start = ((), (), s32[]{:S(2)}) async-start(), calls=%async_computation.9 | async-start | bytes 6553600 | tf_op jit(solution)/shard_map/reduce_scatter | solution.py:209
  1153.6 138.9 %all-reduce.17.cloned.1.call-start = ((), (), s32[]{:S(2)}) async-start(), calls=%async_computation.10 | async-start | bytes 5242880 | tf_op jit(solution)/shard_map/psum | solution.py:232
  1210.0 8.0 copy-start.28
  1218.0 364.7 %all-reduce.19.cloned.1.call-start = ((), (), s32[]{:S(2)}) async-start(), calls=%async_computation.11 | async-start | bytes 29884416 | tf_op jit(solution)/shard_map/psum | solution.py:255
  1218.0 8.0 copy-start.30
  1218.0 8.0 copy-start.65
  1233.7 58.8 %copy-start.45 = (f32[1280]{0:T(1024)S(1)}, f32[1280]{0:T(1024)}, u32[]{:S(2)}) copy-start(f32[1280]{0:T(1024)} %copy-done.44) | copy-start | bytes 15364
  1233.7 58.8 %copy-start.49 = (f32[1024]{0:T(1024)S(1)}, f32[1024]{0:T(1024)}, u32[]{:S(2)}) copy-start(f32[1024]{0:T(1024)} %param.20) | copy-start | bytes 12292
  1308.1 39.4 %copy-start.24 = (bf16[1280,1024,1]{1,0,2:T(8,128)(2,1)S(1)}, bf16[1280,1024,1]{1,0,2:T(8,128)(2,1)}, u32[]{:S(2)}) copy-start(bf16[1280,1024,1]{1,0,2:T(8,128)(2,1)} %copy-done.23) | copy-start | bytes 7864324
  (49 other events, 143.2 us)
Sparse Core Ops, SparseCore 0:
  15.2 133.2 all-reduce.8
  160.5 40.4 all-gather.4
  235.0 40.4 all-gather.2
  446.3 74.7 all-reduce.10
  549.6 74.3 all-reduce.12
  652.3 74.3 all-reduce.14
  1081.4 51.3 reduce-scatter.2
  1153.7 51.3 reduce-scatter.4
  1218.1 74.3 all-reduce.16
  1308.2 274.3 all-reduce.18
where the time goes:
time: 1620 us; the launch traced here: 1610 us
  waiting for transfers between devices  616 us (38%)
  matrix products  551 us (34%)
  other arithmetic  305 us (19%)
  local copies, waits for them, and re-layouts  84.2 us (5%)
  blocking collectives  36.3 us (2%)
    psum x1, waiting for transfers between devices, on_device(): lax.psum(adapter_part.astype(jnp.bfloat16), ('dp', 'seq'))  220 us
    convert_element_type x1, other arithmetic, on_device(): score_grad = (probs_back * (prob_grad - jnp.sum(prob_grad * probs_back, a...  161 us
    dot_general x1, matrix products, on_device(): jnp.einsum('qhd,khd->hqk', attended_back, values_back, preferred_element_...  138 us
    psum x1, waiting for transfers between devices, on_device(): lax.psum(jnp.einsum('rcd,cde->re', latent_embed, adapter, preferred_eleme...  131 us
    dot_general x1, matrix products, score_block(): jnp.einsum('qhd,khd->hqk', queries, keys, preferred_element_type=jnp.floa...  74.7 us
    psum x1, waiting for transfers between devices, on_device(): lax.psum(jnp.dot(attended, output_weight, preferred_element_type=jnp.floa...  74.6 us
    psum x1, waiting for transfers between devices, on_device(): lax.psum(jnp.dot(hidden, down_weight, preferred_element_type=jnp.float32)...  74 us
    dot_general x1, matrix products, on_device(): jnp.einsum('hqk,qhd->khd', probs_back.astype(jnp.bfloat16), attended_back...  71 us
  transfers between devices with their start and end apart: 10, of which 6 were waited for; matrix products, arithmetic and copies ran while one was open for 24% of the time, Pallas kernels for 0%

commit v1 on v0

--- a/solution.py
+++ b/solution.py
@@ -252,7 +252,7 @@
         lax.psum(output_part.astype(jnp.bfloat16), ("dp", "seq")).astype(jnp.float32),
         lax.psum(first_gain_part.astype(jnp.bfloat16), ("dp", "seq")).astype(jnp.float32),
         lax.psum(second_gain_part.astype(jnp.bfloat16), ("dp", "seq")).astype(jnp.float32),
-        lax.psum(adapter_part.astype(jnp.bfloat16), ("dp", "seq")).astype(jnp.float32),
+        lax.psum(lax.psum(adapter_part.astype(jnp.bfloat16), "seq"), "dp").astype(jnp.float32),
     )
     gate_total, up_total, down_total, third_total, fourth_total = (
         summed[0],

time: 1620 us -> 1730 us (1.068)
  waiting for transfers between devices: 616 us -> 727 us
    psum x1 -> x3, waiting for transfers between devices: 220 us -> 299 us  [the longest x1 245 us: on_device(): lax.psum(query_part.astype(jnp.bfloat16), ('dp', 'seq')).astype(jnp.float32)]
    psum x1, waiting for transfers between devices: 56.2 us -> 74.2 us  [on_device(): lax.psum(first_term.astype(jnp.bfloat16), 'tensor').astype(jnp.float32)]
  transfers between devices with their start and end apart: 10 -> 12, of which waited for: 6 -> 8; matrix products, arithmetic and copies ran while one was open for 24% -> 23% of each run, Pallas kernels for 0% -> 0%
where the time goes in v1:
time: 1730 us; the launch traced here: 1720 us
  waiting for transfers between devices  727 us (42%)
  matrix products  551 us (32%)
  other arithmetic  307 us (18%)
  local copies, waits for them, and re-layouts  83.9 us (5%)
  blocking collectives  35.2 us (2%)
    psum x1, waiting for transfers between devices, on_device(): lax.psum(query_part.astype(jnp.bfloat16), ('dp', 'seq')).astype(jnp.float32)  245 us
    convert_element_type x1, other arithmetic, on_device(): score_grad = (probs_back * (prob_grad - jnp.sum(prob_grad * probs_back, a...  161 us
    dot_general x1, matrix products, on_device(): jnp.einsum('qhd,khd->hqk', attended_back, values_back, preferred_element_...  138 us
    psum x1, waiting for transfers between devices, on_device(): lax.psum(jnp.einsum('rcd,cde->re', latent_embed, adapter, preferred_eleme...  131 us
    dot_general x1, matrix products, score_block(): jnp.einsum('qhd,khd->hqk', queries, keys, preferred_element_type=jnp.floa...  74.7 us
    psum x1, waiting for transfers between devices, on_device(): lax.psum(jnp.dot(attended, output_weight, preferred_element_type=jnp.floa...  74.6 us
    psum x1, waiting for transfers between devices, on_device(): lax.psum(third_term.astype(jnp.bfloat16), 'tensor').astype(jnp.float32)  74.2 us
    psum x1, waiting for transfers between devices, on_device(): lax.psum(first_term.astype(jnp.bfloat16), 'tensor').astype(jnp.float32)  74.2 us
  transfers between devices with their start and end apart: 12, of which 8 were waited for; matrix products, arithmetic and copies ran while one was open for 23% of the time, Pallas kernels for 0%

profile of v1, /device:TPU:0, one launch (start us, length us, event | category | flops | bytes accessed | tf_op | source)
XLA Modules:
  0.0 1721.8 jit_solution(2626691891238002628)
XLA Ops:
  7.2 7.8 convolution_bitcast_fusion
  17.1 131.4 %all-reduce.11.cloned.1.call-done = f32[1280,1024]{1,0:T(8,128)} async-done(((f32[1280,1024]{1,0:T(8,128)}), f32[1280,1024]{1,0:T(8,128)}) %all-reduce.11.cloned.1.call-update) | async-done | bytes 5242896 | tf_op jit(solution)/shard_map/psum | solution.py:84
  160.6 16.5 while.13
  180.3 22.2 %gather_fusion.2 = pred[5120,1280]{1,0:T(8,128)(4,1)} fusion(pred[1280,20]{0,1:T(8,128)(4,1)S(1)} %copy.38, s32[5120]{0:T(1024)S(1)} %broadcast_clamp_fusion), kind=kCustom, calls=%fused_computation.2 | custom fusion | bytes 13127680 | tf_op jit(solution)/shard_map/jit(_take)/gather | solution.py:58
  202.5 11.1 fusion.10
  213.6 16.5 copy.39
  235.0 74.7 %fusion.76 = (f32[8,1280]{1,0:T(8,128)}, f32[8,1280,5120]{2,1,0:T(8,128)}) fusion(bf16[5120,8,64]{0,2,1:T(8,128)(2,1)} %all-gather.5.cloned.1.call-done, bf16[1280,8,32]{0,2,1:T(8,128)(2,1)} %get-tuple-element.125, bf16[1280,8,32]{0,2,1:T(8,128)(2,1)S(1)} %copy-done.20, pred[1280,5120]{1,0:T(8,128)(4,1)} %copy.39), kind=kOutput, calls=%fused_computation.170 | convolution fusion | flops 6870784000 | bytes 222863360 | tf_op jit(solution)/shard_map/qhd,khd->hqk/dot_general | solution.py:114
  309.7 63.5 %fusion.3 = f32[8,1280]{1,0:T(8,128)S(1)} fusion(f32[8,1280,5120]{2,1,0:T(8,128)} %get-tuple-element.136, f32[8,1280]{1,0:T(8,128)} %get-tuple-element.135), kind=kLoop, calls=%fused_computation.16 | loop fusion | flops 104847360 | bytes 209797120 | tf_op jit(solution)/shard_map/reduce_sum | solution.py:120
  373.2 68.2 %fusion.56 = bf16[8,64,1280]{2,1,0:T(8,128)(2,1)} fusion(bf16[5120,8,64]{0,2,1:T(8,128)(2,1)} %all-gather.3.cloned.1.call-done, f32[8,1280,5120]{2,1,0:T(8,128)} %get-tuple-element.136, f32[8,1280]{1,0:T(8,128)S(1)} %fusion.3, f32[8,1280]{1,0:T(8,128)S(1)} %copy-done.42), kind=kOutput, calls=%fused_computation.97 | convolution fusion | flops 6868828160 | bytes 216350720 | tf_op jit(solution)/shard_map/hqk,khd->qhd/dot_general | solution.py:123
  446.3 74.6 %all-reduce.13.cloned.1.call-done = bf16[1280,1024]{1,0:T(8,128)(2,1)} async-done(((bf16[1280,1024]{1,0:T(8,128)(2,1)}), bf16[1280,1024]{1,0:T(8,128)(2,1)}) %all-reduce.13.cloned.1.call-update) | async-done | bytes 2621456 | tf_op jit(solution)/shard_map/psum | solution.py:127
  535.3 6.6 multiply_convert_fusion.2
  549.8 74.0 %all-reduce.15.cloned.1.call-done = bf16[1280,1024]{1,0:T(8,128)(2,1)} async-done(((bf16[1280,1024]{1,0:T(8,128)(2,1)}), bf16[1280,1024]{1,0:T(8,128)(2,1)}) %all-reduce.15.cloned.1.call-update) | async-done | bytes 2621456 | tf_op jit(solution)/shard_map/psum | solution.py:138
  630.6 11.4 fusion.14
  646.3 5.7 add_convert_fusion.1
  652.4 74.2 %all-reduce.17.cloned.1.call-done = bf16[1280,1024]{1,0:T(8,128)(2,1)} async-done(((bf16[1280,1024]{1,0:T(8,128)(2,1)}), bf16[1280,1024]{1,0:T(8,128)(2,1)}) %all-reduce.17.cloned.1.call-update) | async-done | bytes 2621456 | tf_op jit(solution)/shard_map/psum | solution.py:166
  726.6 5.6 fusion.52
  732.2 8.5 fusion.47
  744.6 138.2 %multiply_reduce_fusion = (f32[8,1280]{1,0:T(8,128)S(1)}, f32[8,1280,5120]{2,1,0:T(8,128)}) fusion(f32[8,1280,5120]{2,1,0:T(8,128)} %get-tuple-element.136, f32[8,1280]{1,0:T(8,128)S(1)} %log_add_fusion, bf16[1280,8,64]{0,2,1:T(8,128)(2,1)S(1)} %bitcast.82, bf16[5120,8,64]{0,2,1:T(8,128)(2,1)} %all-gather.3.cloned.1.call-done), kind=kOutput, calls=%fused_computation.11 | convolution fusion | flops 6868162560 | bytes 426065920 | tf_op jit(solution)/shard_map/qhd,khd->hqk/dot_general | solution.py:186
  882.9 160.8 %multiply_convert_fusion = bf16[8,1280,5120]{2,1,0:T(8,128)(2,1)} fusion(f32[8,1280,5120]{2,1,0:T(8,128)} %get-tuple-element.140, f32[8,1280,5120]{2,1,0:T(8,128)} %get-tuple-element.136, f32[8,1280]{1,0:T(8,128)S(1)} %get-tuple-element.139, f32[8,1280]{1,0:T(8,128)S(1)} %log_add_fusion), kind=kLoop, calls=%fused_computation.10 | loop fusion | flops 209715200 | bytes 524369920 | tf_op jit(solution)/shard_map/convert_element_type | solution.py:191
  1043.7 37.4 %fusion.55 = bf16[5120,8,64]{0,2,1:T(8,128)(2,1)} fusion(bf16[8,1280,5120]{2,1,0:T(8,128)(2,1)} %multiply_convert_fusion, bf16[1280,8,32]{0,2,1:T(8,128)(2,1)S(1)} %copy-done.22, bf16[1280,8,32]{0,2,1:T(8,128)(2,1)S(1)} %copy-done.21), kind=kOutput, calls=%fused_computation.82 | convolution fusion | flops 6718750720 | bytes 111411200 | tf_op jit(solution)/shard_map/hqk,qhd->khd/dot_general | solution.py:197
  1082.4 71.0 %fusion.19 = bf16[5120,8,64]{0,2,1:T(8,128)(2,1)} fusion(bf16[1280,8,64]{0,2,1:T(8,128)(2,1)S(1)} %bitcast.83, f32[8,1280,5120]{2,1,0:T(8,128)} %get-tuple-element.136, f32[8,1280]{1,0:T(8,128)S(1)} %log_add_fusion), kind=kOutput, calls=%fused_computation.40 | convolution fusion | flops 6818365440 | bytes 216309760 | tf_op jit(solution)/shard_map/hqk,qhd->khd/dot_general | solution.py:199
  1153.4 44.0 %multiply_bitcast_fusion = f32[1280,8,64]{0,2,1:T(8,128)S(1)} fusion(bf16[5120,8,64]{0,2,1:T(8,128)(2,1)} %all-gather.5.cloned.1.call-done, bf16[8,1280,5120]{2,1,0:T(8,128)(2,1)} %multiply_convert_fusion), kind=kOutput, calls=%fused_computation.99 | convolution fusion | flops 6711541760 | bytes 112721920 | tf_op jit(solution)/shard_map/hqk,khd->qhd/dot_general | solution.py:193
  1209.5 7.5 add_convert_fusion
  1217.5 74.2 %all-reduce.19.cloned.1.call-done = bf16[1280,1024]{1,0:T(8,128)(2,1)} async-done(((bf16[1280,1024]{1,0:T(8,128)(2,1)}), bf16[1280,1024]{1,0:T(8,128)(2,1)}) %all-reduce.19.cloned.1.call-update) | async-done | bytes 2621456 | tf_op jit(solution)/shard_map/psum | solution.py:232
  1307.5 8.8 convolution_convert_fusion.3
  1316.3 5.7 convolution_convert_fusion.2
  1322.1 36.8 %all-reduce.21.cloned.1.call-done = bf16[2,512,1024]{1,2,0:T(8,128)(2,1)} async-done(((bf16[2,512,1024]{1,2,0:T(8,128)(2,1)}), bf16[2,512,1024]{1,2,0:T(8,128)(2,1)}) %all-reduce.21.cloned.1.call-update) | async-done | bytes 2097168 | tf_op jit(solution)/shard_map/psum | solution.py:255
  1359.2 8.8 convolution_convert_fusion.4
  1379.0 35.2 %all-reduce = (bf16[1024]{0:T(1024)(128)(2,1)S(1)}, bf16[1024]{0:T(1024)(128)(2,1)S(1)}, bf16[1024]{0:T(1024)(128)(2,1)S(1)}, bf16[1024]{0:T(1024)(128)(2,1)S(1)}) all-reduce(bf16[1024]{0:T(1024)(128)(2,1)S(1)} %get-tuple-element.91, bf16[1024]{0:T(1024)(128)(2,1)S(1)} %copy-done.54, ...), channel_id=1, replica_groups=mesh['dp'=4,'seq'=4,'tensor'=2] {'dp','seq'}, use_global_device_ids=true, to_apply=%region_23.24 | all-reduce | flops 4096 | bytes 16384 | tf_op jit(solution)/shard_map/psum | solution.py:253
  1421.2 10.7 copy.42
  1431.9 16.5 all-reduce.23.cloned.1.call-done
  1452.5 245.2 %all-reduce.25.cloned.1.call-done = (bf16[1024,512]{1,0:T(8,128)(2,1)}, bf16[1024,512]{1,0:T(8,128)(2,1)}, bf16[1024,512]{1,0:T(8,128)(2,1)}, bf16[512,1024]{1,0...) async-done(((bf16[1024,512]{1,0:T(8,128)(2,1)}, bf16[1024,512]{1,0:T(8,128)(2,1)}, bf16[1024,512]{1,0:T(8,128)(2,1)}, ...) | async-done | bytes 12845072 | tf_op jit(solution)/shard_map/psum | solution.py:249
  (347 shorter events, 149.2 us)
Async XLA Ops:
  7.2 536.6 %copy-start = (bf16[1408,1024]{1,0:T(8,128)(2,1)S(1)}, bf16[1408,1024]{1,0:T(8,128)(2,1)}, u32[]{:S(2)}) copy-start(bf16[1408,1024]{1,0:T(8,128)(2,1)} %param.29) | copy-start | bytes 8650756
  7.2 141.2 %all-reduce.11.cloned.1.call-start = ((), (), s32[]{:S(2)}) async-start(), calls=%async_computation.2 | async-start | bytes 10485760 | tf_op jit(solution)/shard_map/psum | solution.py:84
  15.0 136.5 %copy-start.49 = (f32[1024]{0:T(1024)S(1)}, f32[1024]{0:T(1024)}, u32[]{:S(2)}) copy-start(f32[1024]{0:T(1024)} %param.20) | copy-start | bytes 12292
  15.1 219.9 %all-gather.5.cloned.1.call-start = ((), (), s32[]{:S(2)}) async-start(), calls=%async_computation.4 | async-start | bytes 6553600 | tf_op jit(solution)/shard_map/all_gather | solution.py:105
  17.1 140.3 %copy-start.30 = (f32[1280,32]{0,1:T(8,128)}, f32[1280,32]{0,1:T(8,128)S(1)}, u32[]{:S(2)}) copy-start(f32[1280,32]{0,1:T(8,128)S(1)} %get-tuple-element.134) | copy-start | bytes 491524
  160.4 212.8 %all-gather.3.cloned.1.call-start = ((), (), s32[]{:S(2)}) async-start(), calls=%async_computation.3 | async-start | bytes 6553600 | tf_op jit(solution)/shard_map/all_gather | solution.py:106
  234.9 286.0 %all-reduce.13.cloned.1.call-start = ((), (), s32[]{:S(2)}) async-start(), calls=%async_computation.5 | async-start | bytes 5242880 | tf_op jit(solution)/shard_map/psum | solution.py:127
  309.7 63.5 %copy-start.42 = (f32[8,1280]{1,0:T(8,128)S(1)}, f32[8,1280]{1,0:T(8,128)}, u32[]{:S(2)}) copy-start(f32[8,1280]{1,0:T(8,128)} %get-tuple-element.135) | copy-start | bytes 122884
  446.0 77.4 %copy-start.48 = (f32[1024]{0:T(1024)S(1)}, f32[1024]{0:T(1024)}, u32[]{:S(2)}) copy-start(f32[1024]{0:T(1024)} %param.25) | copy-start | bytes 12292
  446.1 177.8 %all-reduce.15.cloned.1.call-start = ((), (), s32[]{:S(2)}) async-start(), calls=%async_computation.6 | async-start | bytes 5242880 | tf_op jit(solution)/shard_map/psum | solution.py:138
  549.3 77.0 %copy-start.51 = (f32[1024]{0:T(1024)S(1)}, f32[1024]{0:T(1024)}, u32[]{:S(2)}) copy-start(f32[1024]{0:T(1024)} %param.30) | copy-start | bytes 12292
  549.3 177.3 %all-reduce.17.cloned.1.call-start = ((), (), s32[]{:S(2)}) async-start(), calls=%async_computation.7 | async-start | bytes 5242880 | tf_op jit(solution)/shard_map/psum | solution.py:166
  626.4 105.8 %copy-start.45 = (f32[1280]{0:T(1024)}, f32[1280]{0:T(1024)S(1)}, u32[]{:S(2)}) copy-start(f32[1280]{0:T(1024)S(1)} %add_rsqrt_fusion) | copy-start | bytes 15364
  630.6 11.4 copy-start.56
  630.6 11.4 copy-start.60
  652.1 545.3 %reduce-scatter.3.cloned.1.call-start = ((), (), s32[]{:S(2)}) async-start(), calls=%async_computation.8 | async-start | bytes 6553600 | tf_op jit(solution)/shard_map/reduce_scatter | solution.py:206
  652.3 79.8 %copy-start.9 = (bf16[1280,1024]{1,0:T(8,128)(2,1)S(1)}, bf16[1280,1024]{1,0:T(8,128)(2,1)}, u32[]{:S(2)}) copy-start(bf16[1280,1024]{1,0:T(8,128)(2,1)} %all-reduce.13.cloned.1.call-done) | copy-start | bytes 7864324
  744.6 138.3 %copy-start.3 = (bf16[1280,512]{0,1:T(8,128)(2,1)}, bf16[1280,512]{0,1:T(8,128)(2,1)S(1)}, u32[]{:S(2)}) copy-start(bf16[1280,512]{0,1:T(8,128)(2,1)S(1)} %convolution_convert_fusion.6) | copy-start | bytes 3932164
  882.9 160.8 %copy-start.21 = (bf16[1280,8,32]{0,2,1:T(8,128)(2,1)S(1)}, bf16[1280,8,32]{0,2,1:T(8,128)(2,1)}, u32[]{:S(2)}) copy-start(bf16[1280,8,32]{0,2,1:T(8,128)(2,1)} %get-tuple-element.124) | copy-start | bytes 1966084
  882.9 160.8 %copy-start.22 = (bf16[1280,8,32]{0,2,1:T(8,128)(2,1)S(1)}, bf16[1280,8,32]{0,2,1:T(8,128)(2,1)}, u32[]{:S(2)}) copy-start(bf16[1280,8,32]{0,2,1:T(8,128)(2,1)} %get-tuple-element.125) | copy-start | bytes 1966084
  1081.1 128.4 %reduce-scatter.5.cloned.1.call-start = ((), (), s32[]{:S(2)}) async-start(), calls=%async_computation.9 | async-start | bytes 6553600 | tf_op jit(solution)/shard_map/reduce_scatter | solution.py:209
  1153.3 138.4 %all-reduce.19.cloned.1.call-start = ((), (), s32[]{:S(2)}) async-start(), calls=%async_computation.10 | async-start | bytes 5242880 | tf_op jit(solution)/shard_map/psum | solution.py:232
  1209.5 82.3 %copy-start.44 = (f32[1280]{0:T(1024)S(1)}, f32[1280]{0:T(1024)}, u32[]{:S(2)}) copy-start(f32[1280]{0:T(1024)} %copy-done.43) | copy-start | bytes 15364
  1209.5 82.3 %copy-start.50 = (f32[1024]{0:T(1024)S(1)}, f32[1024]{0:T(1024)}, u32[]{:S(2)}) copy-start(f32[1024]{0:T(1024)} %param.20) | copy-start | bytes 12292
  1217.0 141.9 %all-reduce.21.cloned.1.call-start = ((), (), s32[]{:S(2)}) async-start(), calls=%async_computation.11 | async-start | bytes 4194304 | tf_op jit(solution)/shard_map/psum | solution.py:255
  1307.3 9.0 copy-start.12
  1307.4 8.9 copy-start.46
  1307.4 8.9 copy-start.52
  1307.4 8.9 copy-start.57
  1307.4 141.0 %all-reduce.23.cloned.1.call-start = ((), (), s32[]{:S(2)}) async-start(), calls=%async_computation.12 | async-start | bytes 4194304 | tf_op jit(solution)/shard_map/psum | solution.py:255
  1358.9 338.7 %all-reduce.25.cloned.1.call-start = ((), (), s32[]{:S(2)}) async-start(), calls=%async_computation.13 | async-start | bytes 25690112 | tf_op jit(solution)/shard_map/psum | solution.py:249
  1378.3 38.3 %copy-start.24 = (bf16[1280,1024,1]{1,0,2:T(8,128)(2,1)S(1)}, bf16[1280,1024,1]{1,0,2:T(8,128)(2,1)}, u32[]{:S(2)}) copy-start(bf16[1280,1024,1]{1,0,2:T(8,128)(2,1)} %copy-done.23) | copy-start | bytes 7864324
  (55 other events, 194.8 us)
Sparse Core Ops, SparseCore 0:
  15.2 133.2 all-reduce.10
  160.5 40.4 all-gather.4
  235.0 40.4 all-gather.2
  446.2 74.6 all-reduce.12
  549.5 74.3 all-reduce.14
  652.2 74.3 all-reduce.16
  1081.2 51.3 reduce-scatter.2
  1153.5 51.3 reduce-scatter.4
  1217.1 74.5 all-reduce.18
  1307.5 51.3 all-reduce.20
  1361.3 87.0 all-reduce.22
  1455.8 241.7 all-reduce.24
